TPU v7x, 32 devices: a whole 2x2x4 slice. The times are simulated.
32 devices in a mesh: groups: 2 (over x), wide: 16 (over z, y, core).
Axes of the slice: x: 2, y: 2, z: 4, core: 2. Of those that a mesh axis runs over, the one named last changes fastest.
Arguments:
- queries: bfloat16 [256, 3072], P(('groups', 'wide')), parts along dimension 0, may hold values from -15 to 15
- hidden_in: bfloat16 [256, 3072], P(('groups', 'wide')), parts along dimension 0, may hold values from -170 to 170
- prefix_keys: bfloat16 [16384, 512], P(('groups', 'wide')), parts along dimension 0, may hold values from -12 to 12
- prefix_values: bfloat16 [16384, 512], P(('groups', 'wide')), parts along dimension 0, may hold values from -24 to 24
- suffix_keys: bfloat16 [256, 64, 512], P(('groups', 'wide')), parts along dimension 0, may hold values from -21 to 21
- suffix_values: bfloat16 [256, 64, 512], P(('groups', 'wide')), parts along dimension 0, may hold values from -24 to 24
- suffix_length: int32 [256], P(('groups', 'wide')), parts along dimension 0, may hold values from 2 to 64, as said below
- prefix_of: int32 [256, 1], P('groups'), parts along dimension 0, may hold values from 0 to 7; in each aligned block of 8 rows (0 to 7, 8 to 15, ...) at most 2 rows name the same one
- expert_index: int32 [256, 2], P('groups'), parts along dimension 0, may hold values from 0 to 3, all different within a row; in each aligned block of 8 rows (0 to 7, 8 to 15, ...) at most 6 rows name the same one
- gate_logits: float32 [256, 2], P('groups'), parts along dimension 0, may hold values from -6 to 6
- norm_gain: float32 [3072], replicated, may hold values from 0.1 to 1.9
- gate_weight: bfloat16 [3072, 32768], P(None, 'wide'), may hold values from -0.109375 to 0.109375
- up_weight: bfloat16 [3072, 32768], P(None, 'wide'), may hold values from -0.109375 to 0.109375
- down_weight: bfloat16 [32768, 3072], P('wide'), may hold values from -0.125 to 0.125
Outputs:
- attended: bfloat16 [256, 3072], P(('groups', 'wide')), parts along dimension 0
- expert_mix: bfloat16 [256, 3072], P(('groups', 'wide')), parts along dimension 0
There are 2 independent parts, one for each index of `groups`. A program takes and returns all parts, laid end to end along the dimension named above; an argument that names none is the same for every part. Nothing has to cross between parts.
Inputs may be any that keep to these rules, and one draw needn't show every extreme that they name: `prefix_of`: among the requests of one device at most 2 share a prefix; in some of the aligned blocks exactly 2 do. `expert_index`: each request names 2 different experts; among the requests of one device at most 6 name the same expert, and in some aligned blocks exactly 6 do. `suffix_length`: every device holds a request with 64 live suffix tokens.
All inputs are finite; a program needn't handle non-finite values.
Results may differ from a plain program's by a relative error of at most 0.0095.
Values may be sent and summed in bfloat16 or wider, within the bound.
A program may use at most 128 MiB of HBM per device.

v0:
```python
import functools
import math

import jax
import jax.numpy as jnp
from jax import lax
from jax.experimental import pallas as pl
from jax.experimental.pallas import tpu as pltpu
from jax.sharding import PartitionSpec as P

HQ = 24
HK = 4
DH = 128
EXPERTS = 4
PREFIXES = 8
CAPP = 2
GROUP = HQ // HK
GPAD = 8

masked_score = -1e30
F32 = jnp.float32
BF16 = jnp.bfloat16


def nt(a, b):
    return lax.dot_general(a, b, (((1,), (1,)), ((), ())), preferred_element_type=F32)


def softmax_block(scores, values):
    top = jnp.max(scores, axis=1, keepdims=True)
    weights = jnp.exp(scores - top).astype(BF16)
    total = jnp.sum(weights.astype(F32), axis=1, keepdims=True)
    out = jnp.dot(weights, values, preferred_element_type=F32)
    return out, top, total


def kernel(
    n,
    len_s,
    pref_s,
    q_hbm,
    hid_hbm,
    pk_hbm,
    pv_hbm,
    sk_hbm,
    sv_hbm,
    ei_hbm,
    gl_hbm,
    gain_hbm,
    wg_hbm,
    wu_hbm,
    wd_hbm,
    att_ref,
    mix_ref,
    q_ref,
    hid_ref,
    sk_ref,
    sv_ref,
    ei_ref,
    gl_ref,
    gain_ref,
    kx,
    vx,
    wg_v,
    wu_v,
    wd_v,
    qsend,
    qrecv,
    pout,
    bout,
    stream,
    x_v,
    h_v,
    dsend,
    drecv,
    keep,
    esend,
    erecv,
    keep2,
    zsend,
    zrecv,
    in_sem,
    w_sem,
    kv_ss,
    kv_rs,
    q_ss,
    q_rs,
    o_ss,
    o_rs,
    x_ss,
    x_rs,
    y_ss,
    f_ss,
    d_ss,
    d_rs,
    e_ss,
    e_rs,
    z_ss,
    z_rs,
):
    me = lax.axis_index("wide")
    rows, width = q_ref.shape
    quads = n // 4
    parity = lax.rem(me, 2)
    half = lax.rem(me // 2, 2)
    quad = me // 4
    sib = me + 1 - 2 * parity
    pair = me + 2 - 4 * half
    heads = HK // 2
    chips_p = n // PREFIXES // 2
    hold_p = n // PREFIXES
    hold_e = n // EXPERTS
    slots = CAPP * GPAD
    up_chunks, _, up_cols = wg_v.shape
    down_chunks, _, down_cols = wd_v.shape
    scale = 1.0 / math.sqrt(DH)

    def send(src, dst, ss, rs, to):
        return pltpu.make_async_remote_copy(
            src_ref=src,
            dst_ref=dst,
            send_sem=ss,
            recv_sem=rs,
            device_id={"wide": to},
            device_id_type=pl.DeviceIdType.MESH,
        )

    barrier = pltpu.get_barrier_semaphore()

    @pl.loop(1, n)
    def _(d):
        pl.semaphore_signal(
            barrier,
            inc=1,
            device_id={"wide": lax.rem(me + d, n)},
            device_id_type=pl.DeviceIdType.MESH,
        )

    ins = [
        pltpu.make_async_copy(src, dst, in_sem.at[i])
        for i, (src, dst) in enumerate(
            (
                (q_hbm, q_ref),
                (sk_hbm, sk_ref),
                (sv_hbm, sv_ref),
                (hid_hbm, hid_ref),
                (ei_hbm, ei_ref),
                (gl_hbm, gl_ref),
                (gain_hbm, gain_ref),
            )
        )
    ]
    for copy in ins:
        copy.start()

    tokens, span = pk_hbm.shape[0], heads * DH
    here = pl.ds(pl.multiple_of(parity * span, span), span)
    there = pl.ds(pl.multiple_of((1 - parity) * span, span), span)
    kv_own = [
        pltpu.make_async_copy(pk_hbm.at[:, here], kx.at[parity], in_sem.at[7]),
        pltpu.make_async_copy(pv_hbm.at[:, here], vx.at[parity], in_sem.at[8]),
    ]
    kv_sib = [
        send(pk_hbm.at[:, there], kx.at[parity], kv_ss.at[0], kv_rs.at[0], sib),
        send(pv_hbm.at[:, there], vx.at[parity], kv_ss.at[1], kv_rs.at[1], sib),
    ]
    for copy in kv_own:
        copy.start()

    def up_copy(j):
        cols = pl.ds(pl.multiple_of(j * up_cols, up_cols), up_cols)
        return (
            pltpu.make_async_copy(wg_hbm.at[:, cols], wg_v.at[j], w_sem.at[0, j]),
            pltpu.make_async_copy(wu_hbm.at[:, cols], wu_v.at[j], w_sem.at[1, j]),
        )

    def down_copy(j):
        cols = pl.ds(pl.multiple_of(j * down_cols, down_cols), down_cols)
        return pltpu.make_async_copy(wd_hbm.at[:, cols], wd_v.at[j], w_sem.at[2, j])

    @pl.loop(0, up_chunks)
    def _(j):
        a, b = up_copy(j)
        a.start()
        b.start()

    @pl.loop(0, down_chunks)
    def _(j):
        down_copy(j).start()

    m = GROUP * rows
    shape = (m, PREFIXES * slots)
    sub = lax.broadcasted_iota(jnp.int32, shape, 0)
    lane = lax.broadcasted_iota(jnp.int32, shape, 1)
    req = lax.rem(sub, rows)
    own = [pref_s[me * rows + j] for j in range(rows)]
    pcol = jnp.zeros(shape, jnp.int32)
    for j in range(rows):
        pcol = jnp.where(req == j, own[j], pcol)
    rank = jnp.zeros(shape, jnp.int32)
    for j in range(rows):
        rank = rank + jnp.where((pcol == own[j]) & (req > j), 1, 0)
    place = pcol * slots + rank * GPAD + lax.div(sub, rows)
    pick_f = jnp.where((lane == place) & (rank < CAPP), 1.0, 0.0)
    pick = pick_f.astype(BF16)

    ins[0].wait()
    q_heads = []
    for k in range(HK):
        parts = [
            q_ref[:, (k * GROUP + g) * DH : (k * GROUP + g + 1) * DH].astype(F32)
            for g in range(GROUP)
        ]
        qk = jnp.concatenate(parts, axis=0).astype(BF16)
        q_heads.append(qk)
        moved = lax.dot_general(
            pick, qk, (((0,), (0,)), ((), ())), preferred_element_type=F32
        )
        qsend[:, k // heads, k % heads] = moved.astype(BF16).reshape(
            PREFIXES, slots, DH
        )

    qrecv[me] = qsend[me // hold_p, parity]
    pl.semaphore_wait(barrier, n - 1)

    def q_copy(d):
        to = lax.rem(me + d, n)
        return send(
            qsend.at[to // hold_p, lax.rem(to, 2)],
            qrecv.at[me],
            q_ss.at[d],
            q_rs.at[me],
            to,
        )

    @pl.loop(1, n)
    def _(d):
        q_copy(d).start()

    for copy in kv_sib:
        copy.start()

    keys = sk_ref.shape[0]
    smax = keys // rows
    s_sub = lax.broadcasted_iota(jnp.int32, (m, keys), 0)
    s_lane = lax.broadcasted_iota(jnp.int32, (m, keys), 1)
    s_req = lax.rem(s_sub, rows)
    limit = jnp.zeros((m, keys), jnp.int32)
    for j in range(rows):
        limit = jnp.where(s_req == j, j * smax + len_s[j], limit)
    usable = (s_lane >= s_req * smax) & (s_lane < limit)
    ins[1].wait()
    ins[2].wait()
    suffix = []
    for k in range(HK):
        head = slice(k * DH, (k + 1) * DH)
        scores = nt(q_heads[k], sk_ref[:, head]) * scale
        scores = jnp.where(usable, scores, masked_score)
        suffix.append(softmax_block(scores, sv_ref[:, head]))

    for copy in ins[3:]:
        copy.wait()
    logits = gl_ref[...]
    e = jnp.exp(logits - jnp.max(logits, axis=0, keepdims=True))
    gates = e / jnp.sum(e, axis=0, keepdims=True)
    mine = ei_ref[...] == me // hold_e
    share = jnp.sum(jnp.where(mine, gates, 0.0), axis=0, keepdims=True)
    share = jnp.broadcast_to(share, (DH, n * rows)).T[:, :1]

    def q_wait(src):
        send(
            qsend.at[0, 0], qrecv.at[src], q_ss.at[0], q_rs.at[src], me
        ).wait_recv()

    @pl.loop(1, n)
    def _(d):
        q_wait(lax.rem(me + d, n))

    for copy in kv_own:
        copy.wait()
    for copy in kv_sib:
        copy.wait_recv()

    total_rows = n * slots
    p_sub = lax.rem(lax.broadcasted_iota(jnp.int32, (total_rows, DH), 0), GPAD)
    p_lane = lax.broadcasted_iota(jnp.int32, (total_rows, DH), 1)
    groups = total_rows // GPAD
    for k in range(heads):
        head = slice(k * DH, (k + 1) * DH)
        queries = qrecv[:, k].reshape(total_rows, DH)
        out, top, total = softmax_block(
            nt(queries, kx[:, :, head].reshape(2 * tokens, DH)) * scale,
            vx[:, :, head].reshape(2 * tokens, DH),
        )
        out = out / total
        log_sum = top + jnp.log(total)
        high = log_sum.astype(BF16).astype(F32)
        rest = log_sum - high
        mid = rest.astype(BF16).astype(F32)
        low = rest - mid

        def row_of(first, second):
            spread = jnp.where(p_lane == p_sub, first, 0.0)
            spread = jnp.where(p_lane == p_sub + GPAD, second, spread)
            summed = jnp.sum(
                spread.reshape(groups, GPAD, DH), axis=1, keepdims=True
            )
            return jnp.broadcast_to(summed, (groups, GPAD, DH)).reshape(
                total_rows, DH
            )

        out = jnp.where(p_sub == GROUP, row_of(high, mid), out)
        out = jnp.where(p_sub == GROUP + 1, row_of(low, jnp.zeros_like(low)), out)
        pout[:, k] = out.astype(BF16).reshape(n, slots, DH)

    def o_copy(d):
        to = lax.rem(me + d, n)
        return send(pout.at[to], bout.at[me], o_ss.at[d], o_rs.at[me], to)

    @pl.loop(1, n)
    def _(d):
        o_copy(d).start()

    bout[me] = pout[me]

    m_sub = lax.div(lax.broadcasted_iota(jnp.int32, (m, DH), 0), rows)
    m_lane = lax.broadcasted_iota(jnp.int32, (m, DH), 1)
    base = pcol * slots + rank * GPAD

    def pick_row(g):
        return jnp.where((lane == base + g) & (rank < CAPP), 1.0, 0.0).astype(BF16)

    pick_a, pick_b = pick_row(GROUP), pick_row(GROUP + 1)
    lanes_a = (m_lane == m_sub) | (m_lane == m_sub + GPAD)
    lanes_b = m_lane == m_sub

    @pl.loop(1, n)
    def _(d):
        src = lax.rem(me + d, n)
        send(pout.at[0], bout.at[src], o_ss.at[0], o_rs.at[src], me).wait_recv()

    for k in range(HK):
        blocks = bout[:, k % heads].reshape(PREFIXES, chips_p, 2, slots, DH)
        out_s, top_s, sum_s = suffix[k]
        outs, logs = [], []
        overall = top_s
        for h in range(chips_p):
            block = blocks[:, h, k // heads].reshape(PREFIXES * slots, DH)
            outs.append(jnp.dot(pick, block, preferred_element_type=F32))
            row_a = jnp.dot(pick_a, block, preferred_element_type=F32)
            row_b = jnp.dot(pick_b, block, preferred_element_type=F32)
            logs.append(
                jnp.sum(
                    jnp.where(lanes_a, row_a, 0.0) + jnp.where(lanes_b, row_b, 0.0),
                    axis=1,
                    keepdims=True,
                )
            )
            overall = jnp.maximum(overall, logs[-1])
        f = jnp.exp(top_s - overall)
        num, den = f * out_s, f * sum_s
        for h in range(chips_p):
            f = jnp.exp(logs[h] - overall)
            num = num + f * outs[h]
            den = den + f
        result = num / den
        for g in range(GROUP):
            cols = slice((k * GROUP + g) * DH, (k * GROUP + g + 1) * DH)
            att = result[g * rows : (g + 1) * rows].astype(BF16)
            att_ref[:, cols] = att
            stream[:, cols] = hid_ref[:, cols].astype(F32) + att.astype(F32)

    s = stream[...]
    mean = jnp.mean(s * s, axis=1, keepdims=True)
    x_v[me] = (s * lax.rsqrt(mean + 1e-05) * gain_ref[...]).astype(BF16)

    def x_copy(d):
        return send(
            x_v.at[me], x_v.at[me], x_ss.at[d], x_rs.at[me], lax.rem(me + 4 * d, n)
        )

    def x_pair(d):
        src = lax.rem(me + 4 * d, n)
        return send(x_v.at[src], x_v.at[src], y_ss.at[d], x_rs.at[src], pair)

    def x_sib(d):
        src = lax.rem(me + 2 * d, n)
        return send(x_v.at[src], x_v.at[src], f_ss.at[d], x_rs.at[src], sib)

    @pl.loop(1, quads)
    def _(d):
        x_copy(d).start()

    x_pair(0).start()
    x_sib(0).start()

    @pl.loop(1, quads)
    def _(i):
        d = quads - i
        x_pair(d).wait_recv()
        x_pair(d).start()
        x_sib(2 * d).start()
        from_pair = x_sib(lax.rem(2 * d + 3 - 2 * half, 2 * quads))
        from_pair.wait_recv()
        from_pair.start()

    from_pair = x_sib(lax.rem(3 - 2 * half, 2 * quads))
    from_pair.wait_recv()
    from_pair.start()

    @pl.loop(0, 2 * quads)
    def _(d):
        src = lax.rem(sib + 2 * d, n)
        send(x_v.at[me], x_v.at[src], f_ss.at[0], x_rs.at[src], sib).wait_recv()

    x = x_v[...].reshape(n * rows, width)

    @pl.loop(0, up_chunks)
    def _(j):
        a, b = up_copy(j)
        a.wait()
        b.wait()
        gate = jnp.dot(x, wg_v[j], preferred_element_type=F32)
        up = jnp.dot(x, wu_v[j], preferred_element_type=F32)
        h_v[j] = (gate / (1.0 + jnp.exp(-gate)) * up).astype(BF16)

    hidden = jnp.concatenate([h_v[j] for j in range(up_chunks)], axis=1)

    def d_copy(j):
        return send(dsend.at[j], drecv.at[j], d_ss.at[j], d_rs.at[j], sib)

    def e_copy(j):
        return send(esend.at[j], erecv.at[j], e_ss.at[j], e_rs.at[j], pair)

    def z_copy(j, d):
        other = lax.rem(quad + d, quads)
        return send(
            zsend.at[j, other],
            zrecv.at[j, quad],
            z_ss.at[j, d],
            z_rs.at[j, quad],
            4 * other + 2 * half + parity,
        )

    def second(j):
        d_copy(j).wait_recv()
        both = keep[j] + drecv[j].astype(F32)
        low = half == 0
        keep2[j] = jnp.where(low, both[:, 0], both[:, 1])
        esend[j] = jnp.where(low, both[:, 1], both[:, 0]).astype(BF16)
        e_copy(j).start()

    def third(j):
        e_copy(j).wait_recv()
        zsend[j] = (keep2[j] + erecv[j].astype(F32)).astype(BF16)

        @pl.loop(1, quads)
        def _(d):
            z_copy(j, d).start()

        zrecv[j, quad] = zsend[j, quad]

    @pl.loop(0, down_chunks)
    def _(j):
        down_copy(j).wait()
        y = jnp.dot(hidden, wd_v[j], preferred_element_type=F32) * share
        y = y.reshape(quads, 2, 2, rows, down_cols)
        even = parity == 0
        keep[j] = jnp.where(even, y[:, :, 0], y[:, :, 1])
        dsend[j] = jnp.where(even, y[:, :, 1], y[:, :, 0]).astype(BF16)
        d_copy(j).start()

        @pl.when(j > 1)
        def _():
            second(j - 2)

    second(down_chunks - 2)
    third(0)
    second(down_chunks - 1)

    @pl.loop(1, down_chunks)
    def _(j):
        third(j)

    for j in range(down_chunks):

        @pl.loop(1, quads)
        def _(d):
            src = lax.rem(quad + d, quads)
            send(
                zsend.at[j, 0], zrecv.at[j, src], z_ss.at[j, 0], z_rs.at[j, src], me
            ).wait_recv()

        total = jnp.sum(zrecv[j].astype(F32), axis=0)
        mix_ref[:, j * down_cols : (j + 1) * down_cols] = total.astype(BF16)

    for copy in kv_sib:
        copy.wait_send()

    @pl.loop(1, n)
    def _(d):
        q_copy(d).wait_send()
        o_copy(d).wait_send()

    @pl.loop(1, quads)
    def _(d):
        x_copy(d).wait_send()

    @pl.loop(0, quads)
    def _(d):
        x_pair(d).wait_send()

    @pl.loop(0, 2 * quads)
    def _(d):
        x_sib(d).wait_send()

    @pl.loop(0, down_chunks)
    def _(j):
        d_copy(j).wait_send()
        e_copy(j).wait_send()

        @pl.loop(1, quads)
        def _(d):
            z_copy(j, d).wait_send()


def hand_over(a_ref, b_ref, c_ref, d_ref):
    c_ref[...] = a_ref[...]
    d_ref[...] = b_ref[...]


def divisor(size, most):
    while size % most:
        most //= 2
    return most


def local(
    queries,
    hidden_in,
    prefix_keys,
    prefix_values,
    suffix_keys,
    suffix_values,
    suffix_length,
    prefix_of,
    expert_index,
    gate_logits,
    norm_gain,
    gate_weight,
    up_weight,
    down_weight,
):
    n = lax.axis_size("wide")
    rows, width = queries.shape
    hidden = gate_weight.shape[1]
    quads, heads = n // 4, HK // 2
    slots = CAPP * GPAD
    up_cols, down_cols = divisor(hidden, 256), divisor(width, 512)
    ups, downs = hidden // up_cols, width // down_cols
    vmem = pl.BlockSpec(memory_space=pltpu.VMEM)
    smem = pl.BlockSpec(memory_space=pltpu.SMEM)
    hbm = pl.BlockSpec(memory_space=pl.ANY)
    dma = pltpu.SemaphoreType.DMA
    kv = suffix_keys.shape[2]
    shapes = (
        jax.ShapeDtypeStruct((rows, width), BF16),
        jax.ShapeDtypeStruct((rows, width), BF16),
    )
    operands = (
        queries,
        hidden_in,
        prefix_keys,
        prefix_values,
        suffix_keys.reshape(-1, kv),
        suffix_values.reshape(-1, kv),
        expert_index.T,
        gate_logits.T,
        norm_gain.reshape(1, -1),
        gate_weight,
        up_weight,
        down_weight,
    )
    landed = [operands[i] for i in (0, 1, 4, 5, 6, 7, 8)]
    pieces = (downs, quads, rows, down_cols)
    pairs = (downs, quads, 2, rows, down_cols)
    mixed = pl.pallas_call(
        functools.partial(kernel, n),
        out_shape=shapes,
        in_specs=[smem] * 2 + [hbm] * 12,
        out_specs=(vmem, vmem),
        scratch_shapes=[pltpu.VMEM(a.shape, a.dtype) for a in landed]
        + [
            pltpu.VMEM((2, prefix_keys.shape[0], heads * DH), BF16),
            pltpu.VMEM((2, prefix_keys.shape[0], heads * DH), BF16),
            pltpu.VMEM((ups, width, up_cols), BF16),
            pltpu.VMEM((ups, width, up_cols), BF16),
            pltpu.VMEM((downs, hidden, down_cols), BF16),
            pltpu.VMEM((PREFIXES, 2, heads, slots, DH), BF16),
            pltpu.VMEM((n, heads, slots, DH), BF16),
            pltpu.VMEM((n, heads, slots, DH), BF16),
            pltpu.VMEM((n, heads, slots, DH), BF16),
            pltpu.VMEM((rows, width), F32),
            pltpu.VMEM((n, rows, width), BF16),
            pltpu.VMEM((ups, n * rows, up_cols), BF16),
            pltpu.VMEM(pairs, BF16),
            pltpu.VMEM(pairs, BF16),
            pltpu.VMEM(pairs, F32),
            pltpu.VMEM(pieces, BF16),
            pltpu.VMEM(pieces, BF16),
            pltpu.VMEM(pieces, F32),
            pltpu.VMEM(pieces, BF16),
            pltpu.VMEM(pieces, BF16),
            dma((9,)),
            dma((3, max(ups, downs))),
            dma((2,)),
            dma((2,)),
            dma((n,)),
            dma((n,)),
            dma((n,)),
            dma((n,)),
            dma((quads,)),
            dma((n,)),
            dma((quads,)),
            dma((2 * quads,)),
            dma((downs,)),
            dma((downs,)),
            dma((downs,)),
            dma((downs,)),
            dma((downs, quads)),
            dma((downs, quads)),
        ],
        compiler_params=pltpu.CompilerParams(
            collective_id=0, has_side_effects=True, vmem_limit_bytes=63000 * 1024
        ),
    )(suffix_length, prefix_of.reshape(-1), *operands)
    return tuple(
        pl.pallas_call(
            hand_over, out_shape=shapes, in_specs=[vmem] * 2, out_specs=(vmem, vmem)
        )(*mixed)
    )


def solution(mesh):
    placed = (
        P(("groups", "wide"), None),
        P(("groups", "wide"), None),
        P(("groups", "wide"), None),
        P(("groups", "wide"), None),
        P(("groups", "wide"), None, None),
        P(("groups", "wide"), None, None),
        P(("groups", "wide")),
        P("groups", None),
        P("groups", None),
        P("groups", None),
        P(),
        P(None, "wide"),
        P(None, "wide"),
        P("wide", None),
    )
    return jax.shard_map(
        local,
        mesh=mesh,
        in_specs=placed,
        out_specs=(P(("groups", "wide"), None), P(("groups", "wide"), None)),
        check_vma=False,
    )
```

profile of v0, /device:TPU:0, one launch (start us, length us, event | category | flops | bytes accessed | tf_op | source)
XLA Modules:
  0.0 52.0 jit_solution(12490484052881126765)
XLA Ops:
  0.6 49.9 %shard_map.149 = (bf16[8,3072]{1,0:T(8,128)(2,1)}, bf16[8,3072]{1,0:T(8,128)(2,1)}) custom-call(s32[8]{0:T(128)} %len_s.1, s32[128]{0:T(128)} %bitcast.11, bf16[8,3072]{1,0:T(8,128)(2,1)} %q_hbm.1, bf16[8,3072]{1,0:T(8,128)(2,1)} %hid_hbm.1, bf16[512,512]{1,0:T(8,128)(2,1)} %pk_hbm.1, bf16[512,512]{1,0:T(8,128)(2,1)} %pv_hbm.1, bf16[512,512]{1,0:T(8,128)(2,1)} %bitcast.6, ...), custom_call_target="tpu_custom_call" | custom-call | tf_op jit(solution)/shard_map/pallas_call | solution.py:587
  50.5 1.5 %shard_map.150 = (bf16[8,3072]{1,0:T(8,128)(2,1)}, bf16[8,3072]{1,0:T(8,128)(2,1)}) custom-call(bf16[8,3072]{1,0:T(8,128)(2,1)} %get-tuple-element.4.a_ref, bf16[8,3072]{1,0:T(8,128)(2,1)} %get-tuple-element.5.b_ref), custom_call_target="tpu_custom_call" | custom-call | tf_op jit(solution)/shard_map/pallas_call | solution.py:638
where the time goes:
time: 52.2 us; the launch traced here: 52 us
  Pallas kernels  51.4 us (98%)
  between operations  0.64 us (1%)
    pallas_call x1, Pallas kernels, local(): pl.pallas_call(functools.partial(kernel, n), out_shape=shapes, in_specs=[...  49.9 us
    pallas_call x1, Pallas kernels, local(): pl.pallas_call(hand_over, out_shape=shapes, in_specs=[vmem] * 2, out_spec...  1.46 us

commit v1 on v0

--- a/solution.py
+++ b/solution.py
@@ -36,8 +36,8 @@
 
 def kernel(
     n,
-    len_s,
-    pref_s,
+    len_hbm,
+    pref_hbm,
     q_hbm,
     hid_hbm,
     pk_hbm,
@@ -79,8 +79,11 @@
     keep2,
     zsend,
     zrecv,
+    len_s,
+    pref_s,
     in_sem,
     w_sem,
+    kv_in,
     kv_ss,
     kv_rs,
     q_ss,
@@ -89,8 +92,7 @@
     o_rs,
     x_ss,
     x_rs,
-    y_ss,
-    f_ss,
+    g_rs,
     d_ss,
     d_rs,
     e_ss,
@@ -115,6 +117,8 @@
     down_chunks, _, down_cols = wd_v.shape
     scale = 1.0 / math.sqrt(DH)
 
+    others, other_quads = pl.ds(0, n - 1), pl.ds(0, quads - 1)
+
     def send(src, dst, ss, rs, to):
         return pltpu.make_async_remote_copy(
             src_ref=src,
@@ -127,14 +131,43 @@
 
     barrier = pltpu.get_barrier_semaphore()
 
-    @pl.loop(1, n)
-    def _(d):
+    upper = quad // (quads // 2)
+
+    def far_quad(i):
+        down = quads - 1 - i
+        down = down - (quad - down + quads) // quads
+        rise = i + (i - quad + quads) // quads
+        return (1 - upper) * down + upper * rise
+
+    def near_quad(i):
+        return far_quad(quads - 2 - i)
+
+    def for_others(act):
+        @pl.loop(0, quads - 1)
+        def _(i):
+            first = 4 * far_quad(i)
+            for k in range(4):
+                act(first + lax.rem(2 * (1 - half) + k, 4))
+
+        act(pair + 1 - 2 * parity)
+        act(pair)
+        act(sib)
+
+    def greet(to):
         pl.semaphore_signal(
             barrier,
             inc=1,
-            device_id={"wide": lax.rem(me + d, n)},
+            device_id={"wide": to},
             device_id_type=pl.DeviceIdType.MESH,
         )
+
+    for_others(greet)
+    scalars = [
+        pltpu.make_async_copy(pref_hbm, pref_s, in_sem.at[7]),
+        pltpu.make_async_copy(len_hbm, len_s, in_sem.at[8]),
+    ]
+    for copy in scalars:
+        copy.start()
 
     ins = [
         pltpu.make_async_copy(src, dst, in_sem.at[i])
@@ -157,12 +190,12 @@
     here = pl.ds(pl.multiple_of(parity * span, span), span)
     there = pl.ds(pl.multiple_of((1 - parity) * span, span), span)
     kv_own = [
-        pltpu.make_async_copy(pk_hbm.at[:, here], kx.at[parity], in_sem.at[7]),
-        pltpu.make_async_copy(pv_hbm.at[:, here], vx.at[parity], in_sem.at[8]),
+        pltpu.make_async_copy(pk_hbm.at[:, here], kx.at[parity], kv_in),
+        pltpu.make_async_copy(pv_hbm.at[:, here], vx.at[parity], kv_in),
     ]
     kv_sib = [
-        send(pk_hbm.at[:, there], kx.at[parity], kv_ss.at[0], kv_rs.at[0], sib),
-        send(pv_hbm.at[:, there], vx.at[parity], kv_ss.at[1], kv_rs.at[1], sib),
+        send(pk_hbm.at[:, there], kx.at[parity], kv_ss, kv_rs, sib),
+        send(pv_hbm.at[:, there], vx.at[parity], kv_ss, kv_rs, sib),
     ]
     for copy in kv_own:
         copy.start()
@@ -170,13 +203,13 @@
     def up_copy(j):
         cols = pl.ds(pl.multiple_of(j * up_cols, up_cols), up_cols)
         return (
-            pltpu.make_async_copy(wg_hbm.at[:, cols], wg_v.at[j], w_sem.at[0, j]),
-            pltpu.make_async_copy(wu_hbm.at[:, cols], wu_v.at[j], w_sem.at[1, j]),
+            pltpu.make_async_copy(wg_hbm.at[:, cols], wg_v.at[j], w_sem.at[0]),
+            pltpu.make_async_copy(wu_hbm.at[:, cols], wu_v.at[j], w_sem.at[1]),
         )
 
     def down_copy(j):
         cols = pl.ds(pl.multiple_of(j * down_cols, down_cols), down_cols)
-        return pltpu.make_async_copy(wd_hbm.at[:, cols], wd_v.at[j], w_sem.at[2, j])
+        return pltpu.make_async_copy(wd_hbm.at[:, cols], wd_v.at[j], w_sem.at[2])
 
     @pl.loop(0, up_chunks)
     def _(j):
@@ -188,6 +221,8 @@
     def _(j):
         down_copy(j).start()
 
+    for copy in scalars:
+        copy.wait()
     m = GROUP * rows
     shape = (m, PREFIXES * slots)
     sub = lax.broadcasted_iota(jnp.int32, shape, 0)
@@ -223,19 +258,16 @@
     qrecv[me] = qsend[me // hold_p, parity]
     pl.semaphore_wait(barrier, n - 1)
 
-    def q_copy(d):
-        to = lax.rem(me + d, n)
+    def q_copy(to):
         return send(
             qsend.at[to // hold_p, lax.rem(to, 2)],
             qrecv.at[me],
-            q_ss.at[d],
-            q_rs.at[me],
+            q_ss,
+            q_rs,
             to,
         )
 
-    @pl.loop(1, n)
-    def _(d):
-        q_copy(d).start()
+    for_others(lambda to: q_copy(to).start())
 
     for copy in kv_sib:
         copy.start()
@@ -267,19 +299,10 @@
     share = jnp.sum(jnp.where(mine, gates, 0.0), axis=0, keepdims=True)
     share = jnp.broadcast_to(share, (DH, n * rows)).T[:, :1]
 
-    def q_wait(src):
-        send(
-            qsend.at[0, 0], qrecv.at[src], q_ss.at[0], q_rs.at[src], me
-        ).wait_recv()
-
-    @pl.loop(1, n)
-    def _(d):
-        q_wait(lax.rem(me + d, n))
-
-    for copy in kv_own:
-        copy.wait()
-    for copy in kv_sib:
-        copy.wait_recv()
+    send(qrecv.at[others], qrecv.at[others], q_ss, q_rs, sib).wait_recv()
+
+    pltpu.make_async_copy(kx, kx, kv_in).wait()
+    send(kx, kx, kv_ss, kv_rs, sib).wait_recv()
 
     total_rows = n * slots
     p_sub = lax.rem(lax.broadcasted_iota(jnp.int32, (total_rows, DH), 0), GPAD)
@@ -313,13 +336,10 @@
         out = jnp.where(p_sub == GROUP + 1, row_of(low, jnp.zeros_like(low)), out)
         pout[:, k] = out.astype(BF16).reshape(n, slots, DH)
 
-    def o_copy(d):
-        to = lax.rem(me + d, n)
-        return send(pout.at[to], bout.at[me], o_ss.at[d], o_rs.at[me], to)
-
-    @pl.loop(1, n)
-    def _(d):
-        o_copy(d).start()
+    def o_copy(to):
+        return send(pout.at[to], bout.at[me], o_ss, o_rs, to)
+
+    for_others(lambda to: o_copy(to).start())
 
     bout[me] = pout[me]
 
@@ -334,10 +354,7 @@
     lanes_a = (m_lane == m_sub) | (m_lane == m_sub + GPAD)
     lanes_b = m_lane == m_sub
 
-    @pl.loop(1, n)
-    def _(d):
-        src = lax.rem(me + d, n)
-        send(pout.at[0], bout.at[src], o_ss.at[0], o_rs.at[src], me).wait_recv()
+    send(bout.at[others], bout.at[others], o_ss, o_rs, sib).wait_recv()
 
     for k in range(HK):
         blocks = bout[:, k % heads].reshape(PREFIXES, chips_p, 2, slots, DH)
@@ -374,71 +391,63 @@
     mean = jnp.mean(s * s, axis=1, keepdims=True)
     x_v[me] = (s * lax.rsqrt(mean + 1e-05) * gain_ref[...]).astype(BF16)
 
-    def x_copy(d):
-        return send(
-            x_v.at[me], x_v.at[me], x_ss.at[d], x_rs.at[me], lax.rem(me + 4 * d, n)
-        )
-
-    def x_pair(d):
-        src = lax.rem(me + 4 * d, n)
-        return send(x_v.at[src], x_v.at[src], y_ss.at[d], x_rs.at[src], pair)
-
-    def x_sib(d):
-        src = lax.rem(me + 2 * d, n)
-        return send(x_v.at[src], x_v.at[src], f_ss.at[d], x_rs.at[src], sib)
-
-    @pl.loop(1, quads)
-    def _(d):
-        x_copy(d).start()
-
-    x_pair(0).start()
-    x_sib(0).start()
-
-    @pl.loop(1, quads)
-    def _(i):
-        d = quads - i
-        x_pair(d).wait_recv()
-        x_pair(d).start()
-        x_sib(2 * d).start()
-        from_pair = x_sib(lax.rem(2 * d + 3 - 2 * half, 2 * quads))
-        from_pair.wait_recv()
-        from_pair.start()
-
-    from_pair = x_sib(lax.rem(3 - 2 * half, 2 * quads))
-    from_pair.wait_recv()
-    from_pair.start()
-
-    @pl.loop(0, 2 * quads)
-    def _(d):
-        src = lax.rem(sib + 2 * d, n)
-        send(x_v.at[me], x_v.at[src], f_ss.at[0], x_rs.at[src], sib).wait_recv()
+    def x_copy(i):
+        to = 4 * far_quad(i) + 2 * half + parity
+        return send(x_v.at[me], x_v.at[me], x_ss, x_rs.at[me // 2], to)
+
+    def x_pair(src):
+        return send(x_v.at[src], x_v.at[src], x_ss, x_rs.at[src // 2], pair)
+
+    def x_sib(src):
+        return send(x_v.at[src], x_v.at[src], x_ss, g_rs, sib)
+
+    for i in range(quads - 1):
+        x_copy(i).start()
+    x_pair(me).start()
+    x_sib(me).start()
+
+    def from_pair(src):
+        x_pair(src).wait_recv()
+        x_sib(src).start()
+
+    for i in range(quads - 1):
+        src = 4 * near_quad(i) + 2 * half + parity
+        x_pair(src).wait_recv()
+        x_pair(src).start()
+        x_sib(src).start()
+        before = pair if i == 0 else 4 * near_quad(i - 1) + 2 * (1 - half) + parity
+        from_pair(before)
+    from_pair(4 * near_quad(quads - 2) + 2 * (1 - half) + parity)
+
+    landed = x_v.at[pl.ds(0, 2 * quads)]
+    send(landed, landed, x_ss, g_rs, sib).wait_recv()
 
     x = x_v[...].reshape(n * rows, width)
+    pltpu.make_async_copy(wg_v, wg_v, w_sem.at[0]).wait()
+    pltpu.make_async_copy(wu_v, wu_v, w_sem.at[1]).wait()
 
     @pl.loop(0, up_chunks)
     def _(j):
-        a, b = up_copy(j)
-        a.wait()
-        b.wait()
         gate = jnp.dot(x, wg_v[j], preferred_element_type=F32)
         up = jnp.dot(x, wu_v[j], preferred_element_type=F32)
         h_v[j] = (gate / (1.0 + jnp.exp(-gate)) * up).astype(BF16)
 
+    pltpu.make_async_copy(wd_v, wd_v, w_sem.at[2]).wait()
     hidden = jnp.concatenate([h_v[j] for j in range(up_chunks)], axis=1)
 
     def d_copy(j):
-        return send(dsend.at[j], drecv.at[j], d_ss.at[j], d_rs.at[j], sib)
+        return send(dsend.at[j], drecv.at[j], d_ss, d_rs.at[j], sib)
 
     def e_copy(j):
-        return send(esend.at[j], erecv.at[j], e_ss.at[j], e_rs.at[j], pair)
+        return send(esend.at[j], erecv.at[j], e_ss, e_rs.at[j], pair)
 
     def z_copy(j, d):
         other = lax.rem(quad + d, quads)
         return send(
             zsend.at[j, other],
             zrecv.at[j, quad],
-            z_ss.at[j, d],
-            z_rs.at[j, quad],
+            z_ss,
+            z_rs.at[j],
             4 * other + 2 * half + parity,
         )
 
@@ -462,7 +471,6 @@
 
     @pl.loop(0, down_chunks)
     def _(j):
-        down_copy(j).wait()
         y = jnp.dot(hidden, wd_v[j], preferred_element_type=F32) * share
         y = y.reshape(quads, 2, 2, rows, down_cols)
         even = parity == 0
@@ -483,45 +491,19 @@
         third(j)
 
     for j in range(down_chunks):
-
-        @pl.loop(1, quads)
-        def _(d):
-            src = lax.rem(quad + d, quads)
-            send(
-                zsend.at[j, 0], zrecv.at[j, src], z_ss.at[j, 0], z_rs.at[j, src], me
-            ).wait_recv()
-
+        arrived = zrecv.at[j, other_quads]
+        send(arrived, arrived, z_ss, z_rs.at[j], sib).wait_recv()
         total = jnp.sum(zrecv[j].astype(F32), axis=0)
         mix_ref[:, j * down_cols : (j + 1) * down_cols] = total.astype(BF16)
 
-    for copy in kv_sib:
-        copy.wait_send()
-
-    @pl.loop(1, n)
-    def _(d):
-        q_copy(d).wait_send()
-        o_copy(d).wait_send()
-
-    @pl.loop(1, quads)
-    def _(d):
-        x_copy(d).wait_send()
-
-    @pl.loop(0, quads)
-    def _(d):
-        x_pair(d).wait_send()
-
-    @pl.loop(0, 2 * quads)
-    def _(d):
-        x_sib(d).wait_send()
-
-    @pl.loop(0, down_chunks)
-    def _(j):
-        d_copy(j).wait_send()
-        e_copy(j).wait_send()
-
-        @pl.loop(1, quads)
-        def _(d):
-            z_copy(j, d).wait_send()
+    send(kx, kx, kv_ss, kv_rs, sib).wait_send()
+    send(qrecv.at[others], qrecv.at[others], q_ss, q_rs, sib).wait_send()
+    send(bout.at[others], bout.at[others], o_ss, o_rs, sib).wait_send()
+    send(x_v.at[others], x_v.at[others], x_ss, g_rs, sib).wait_send()
+    send(dsend, drecv, d_ss, d_rs.at[0], sib).wait_send()
+    send(esend, erecv, e_ss, e_rs.at[0], sib).wait_send()
+    z_all = zsend.at[:, other_quads]
+    send(z_all, z_all, z_ss, z_rs.at[0], sib).wait_send()
 
 
 def hand_over(a_ref, b_ref, c_ref, d_ref):
@@ -559,14 +541,14 @@
     up_cols, down_cols = divisor(hidden, 256), divisor(width, 512)
     ups, downs = hidden // up_cols, width // down_cols
     vmem = pl.BlockSpec(memory_space=pltpu.VMEM)
-    smem = pl.BlockSpec(memory_space=pltpu.SMEM)
-    hbm = pl.BlockSpec(memory_space=pl.ANY)
+    hbm = pl.BlockSpec(memory_space=pltpu.HBM)
     dma = pltpu.SemaphoreType.DMA
     kv = suffix_keys.shape[2]
     shapes = (
         jax.ShapeDtypeStruct((rows, width), BF16),
         jax.ShapeDtypeStruct((rows, width), BF16),
     )
+    landing = tuple(pltpu.VMEM(a.shape, a.dtype) for a in shapes)
     operands = (
         queries,
         hidden_in,
@@ -582,12 +564,16 @@
         down_weight,
     )
     landed = [operands[i] for i in (0, 1, 4, 5, 6, 7, 8)]
+    placed = [
+        pltpu.with_memory_space_constraint(a, pltpu.HBM)
+        for a in (suffix_length, prefix_of.reshape(-1), *operands)
+    ]
     pieces = (downs, quads, rows, down_cols)
     pairs = (downs, quads, 2, rows, down_cols)
     mixed = pl.pallas_call(
         functools.partial(kernel, n),
-        out_shape=shapes,
-        in_specs=[smem] * 2 + [hbm] * 12,
+        out_shape=landing,
+        in_specs=[hbm] * 14,
         out_specs=(vmem, vmem),
         scratch_shapes=[pltpu.VMEM(a.shape, a.dtype) for a in landed]
         + [
@@ -611,32 +597,38 @@
             pltpu.VMEM(pieces, F32),
             pltpu.VMEM(pieces, BF16),
             pltpu.VMEM(pieces, BF16),
+            pltpu.SMEM(suffix_length.shape, jnp.int32),
+            pltpu.SMEM((prefix_of.size,), jnp.int32),
             dma((9,)),
-            dma((3, max(ups, downs))),
-            dma((2,)),
-            dma((2,)),
-            dma((n,)),
-            dma((n,)),
-            dma((n,)),
-            dma((n,)),
-            dma((quads,)),
-            dma((n,)),
-            dma((quads,)),
-            dma((2 * quads,)),
+            dma((3,)),
+            dma,
+            dma,
+            dma,
+            dma,
+            dma,
+            dma,
+            dma,
+            dma,
+            dma((n // 2,)),
+            dma,
+            dma,
             dma((downs,)),
+            dma,
             dma((downs,)),
+            dma,
             dma((downs,)),
-            dma((downs,)),
-            dma((downs, quads)),
-            dma((downs, quads)),
         ],
         compiler_params=pltpu.CompilerParams(
-            collective_id=0, has_side_effects=True, vmem_limit_bytes=63000 * 1024
+            collective_id=0, has_side_effects=True, vmem_limit_bytes=52 * 2**20
         ),
-    )(suffix_length, prefix_of.reshape(-1), *operands)
+    )(*placed)
     return tuple(
         pl.pallas_call(
-            hand_over, out_shape=shapes, in_specs=[vmem] * 2, out_specs=(vmem, vmem)
+            hand_over,
+            out_shape=shapes,
+            in_specs=[vmem] * 2,
+            out_specs=(vmem, vmem),
+            compiler_params=pltpu.CompilerParams(vmem_limit_bytes=2**20),
         )(*mixed)
     )
 

time: 52.2 us -> 47 us (0.900)
  Pallas kernels: 51.4 us -> 46.2 us
    pallas_call x1, Pallas kernels: 49.9 us -> 45.6 us  [local(): pl.pallas_call(functools.partial(kernel, n), out_shape=landing, in_specs=...]
    pallas_call x1, Pallas kernels: 1.46 us -> 0.64 us  [local(): pl.pallas_call(hand_over, out_shape=shapes, in_specs=[vmem] * 2, out_spec...]
where the time goes in v1:
time: 47 us; the launch traced here: 46.8 us
  Pallas kernels  46.2 us (98%)
  between operations  0.64 us (1%)
    pallas_call x1, Pallas kernels, local(): pl.pallas_call(functools.partial(kernel, n), out_shape=landing, in_specs=...  45.6 us

profile of v1, /device:TPU:0, one launch (start us, length us, event | category | flops | bytes accessed | tf_op | source)
XLA Modules:
  0.0 46.8 jit_solution(10728817484435355418)
XLA Ops:
  0.6 45.6 %shard_map.149 = (bf16[8,3072]{1,0:T(8,128)(2,1)S(1)}, bf16[8,3072]{1,0:T(8,128)(2,1)S(1)}) custom-call(s32[8]{0:T(128)} %len_hbm.1, s32[128]{0:T(128)} %bitcast.11, bf16[8,3072]{1,0:T(8,128)(2,1)} %q_hbm.1, bf16[8,3072]{1,0:T(8,128)(2,1)} %hid_hbm.1, bf16[512,512]{1,0:T(8,128)(2,1)} %pk_hbm.1, bf16[512,512]{1,0:T(8,128)(2,1)} %pv_hbm.1, ...), custom_call_target="tpu_custom_call" | custom-call | tf_op jit(solution)/shard_map/pallas_call | solution.py:573
  46.2 0.6 %shard_map.150 = (bf16[8,3072]{1,0:T(8,128)(2,1)}, bf16[8,3072]{1,0:T(8,128)(2,1)}) custom-call(bf16[8,3072]{1,0:T(8,128)(2,1)S(1)} %get-tuple-element.4.a_ref, bf16[8,3072]{1,0:T(8,128)(2,1)S(1)} %get-tuple-element.5.b_ref), custom_call_target="tpu_custom_call" | custom-call | tf_op jit(solution)/shard_map/pallas_call | solution.py:626
